TPU v7x, 32 devices: a whole 2x2x4 slice. The times are simulated.
32 devices in a mesh: dp: 8 (over z, x), mp: 4 (over y, core).
Axes of the slice: x: 2, y: 2, z: 4, core: 2. Of those that a mesh axis runs over, the one named last changes fastest.
Arguments:
- activations: bfloat16 [1024, 1024], P('dp'), may hold values from -6 to 6
- cotangents: bfloat16 [1024, 4096], P('dp', 'mp'), may hold values from -1200 to 1200
- owners: int32 [4], replicated, may hold values from 0 to 7, as said below
Outputs:
- update: bfloat16 [1024, 4096], P('dp', 'mp')
- roots: float32 [4096, 2048], P('dp', 'mp')
- graft: float32 [], replicated
Inputs may be any that keep to these rules, and one draw needn't show every extreme that they name: The left root of block b is computed at dp index owners[b] and its right root at owners[b] with its lowest bit flipped; every dp index computes exactly one root.
All inputs are finite; a program needn't handle non-finite values.
Results may differ from a plain program's by a relative error of at most 0.00045.
Values may be sent and summed in bfloat16 or wider, within the bound.
No kernel may reach another device: no remote copies, remote signals or barrier semaphores. Data moves between devices by JAX's collectives and lax.ppermute only.
A program may use at most 64 MiB of HBM per device.

v0:
```python
import math
import jax
import jax.numpy as jnp
from jax import lax
from jax.sharding import PartitionSpec as P

B = 512
CB = 2
ITERS = 3


def partner_2(value, axis, bit):
    return lax.ppermute(value, axis, [(i, i ^ 1 << bit) for i in range(lax.axis_size(axis))])


def product(left, right):
    return jnp.dot(left, right, precision=lax.Precision.HIGHEST, preferred_element_type=jnp.float32)


def statistic_of(operand):
    gram = product(operand, operand.T)
    ridge = 0.1 * (jnp.sum(operand * operand) / operand.shape[0] + 1.0)
    return gram + ridge * jnp.eye(operand.shape[0], dtype=jnp.float32)


def inverse_root(statistic):
    eye_matrix = jnp.eye(statistic.shape[0], dtype=jnp.float32)
    magnitude = jnp.sqrt(jnp.sum(statistic * statistic))
    current = statistic / magnitude
    result = eye_matrix
    for step in range(ITERS):
        factor = (5.0 * eye_matrix - current) * 0.25
        if step == 0:
            result = factor * magnitude ** (-0.25)
        else:
            result = product(result, factor)
        if step + 1 < ITERS:
            square = product(factor, factor)
            current = product(product(square, square), current)
    return result


def half_squares(matrix, upper_half):
    row_ids = jnp.arange(matrix.shape[0], dtype=jnp.int32)
    in_half = (row_ids < matrix.shape[0] // 2) == upper_half
    return jnp.sum(jnp.where(in_half[:, None], matrix * matrix, 0.0), axis=0)


def on_device(activations, cotangents, owners):
    my_index = lax.axis_index("dp")
    dp_count = lax.axis_size("dp")
    local_tokens = activations.shape[0]
    row_blocks = activations.shape[1] // B
    block_count = owners.shape[0]
    dest_index = jnp.arange(dp_count, dtype=jnp.int32)
    partner = owners + 1 - 2 * (owners % 2)
    left_match = owners[None, :] == dest_index[:, None]
    right_match = partner[None, :] == dest_index[:, None]
    block_ids = jnp.arange(block_count, dtype=jnp.int32)
    owned = jnp.sum(jnp.where(left_match | right_match, block_ids[None, :], 0), axis=1)
    left_dest = jnp.any(left_match, axis=1)
    row_dest = owned // CB
    col_dest = owned % CB
    my_block = owned[my_index]
    my_left = left_dest[my_index]
    token_rows = jnp.take(activations.reshape(local_tokens, row_blocks, B), row_dest, axis=1)
    cotangent_rows = jnp.take(cotangents.reshape(local_tokens, CB, B), col_dest, axis=1)
    mixed = jnp.where(left_dest[None, :, None], token_rows, cotangent_rows)
    received = lax.all_to_all(mixed, "dp", split_axis=1, concat_axis=0, tiled=True)[:, 0, :]
    partner_part = partner_2(received, "dp", 0)
    inputs_block = jnp.where(my_left, received, partner_part)
    outputs_block = jnp.where(my_left, partner_part, received)
    all_tokens = inputs_block.shape[0]
    gradient = lax.dot_general(
        inputs_block, outputs_block, (((0,), (0,)), ((), ())), preferred_element_type=jnp.float32
    ) / math.sqrt(all_tokens)
    grad_share = half_squares(gradient, my_left)
    grad_total = jnp.sum(lax.psum(grad_share, ("dp", "mp")))
    oriented = jnp.where(my_left, gradient, gradient.T)
    root = inverse_root(statistic_of(oriented))
    other_root = partner_2(root, "dp", 0)
    left_root = jnp.where(my_left, root, other_root)
    right_root = jnp.where(my_left, other_root, root)
    preconditioned = product(left_root, product(gradient, right_root))
    precond_share = half_squares(preconditioned, my_left)
    precond_total = jnp.sum(lax.psum(precond_share, ("dp", "mp")))
    graft = jnp.sqrt(grad_total / jnp.maximum(precond_total, 1.0))
    scaled = jnp.where(my_left, graft * preconditioned, 0.0).astype(jnp.bfloat16)
    dest_rows = activations.shape[1] // dp_count
    pieces = scaled.reshape(B // dest_rows, dest_rows, B)
    outgoing = jnp.zeros((dp_count, dest_rows, B), jnp.bfloat16)
    first_dest = my_block // CB * (B // dest_rows)
    outgoing = lax.dynamic_update_slice(outgoing, pieces, (first_dest, jnp.int32(0), jnp.int32(0)))
    incoming = lax.all_to_all(outgoing, "dp", split_axis=0, concat_axis=0, tiled=True)
    selector = (
        (col_dest[:, None] == jnp.arange(CB, dtype=jnp.int32)[None, :]) & left_dest[:, None]
    ).astype(jnp.bfloat16)
    update = jnp.einsum("srb,sc->rcb", incoming, selector, preferred_element_type=jnp.float32)
    update = update.reshape(dest_rows, CB * B).astype(jnp.bfloat16)
    return (update, root, graft)


def solution(mesh):
    return jax.shard_map(
        on_device,
        mesh=mesh,
        in_specs=(P("dp", None), P("dp", "mp"), P()),
        out_specs=(P("dp", "mp"), P("dp", "mp"), P()),
        check_vma=False,
    )
```

profile of v0, /device:TPU:0, one launch (start us, length us, event | category | flops | bytes accessed | tf_op | source)
XLA Modules:
  0.0 190.2 jit_solution(12887503934430091397)
XLA Ops:
  0.6 0.7 fusion.38
  1.6 1.1 copy.24
  2.9 0.8 copy-done.3
  4.0 0.6 gather_fusion.1
  4.6 0.6 gather_fusion
  5.5 32.8 %all_to_all.20 = bf16[128,8,512]{2,0,1:T(8,128)(2,1)S(1)} all-to-all(bf16[128,8,512]{2,0,1:T(8,128)(2,1)S(1)} %bitcast_select_fusion.1), channel_id=1, replica_groups=mesh['dp'=8,'mp'=4] {'dp'}, dimensions={1} | all-to-all | bytes 2097152 | tf_op jit(solution)/shard_map/all_to_all | solution.py:69
  38.3 1.4 collective-permute-start
  39.8 0.6 dynamic_slice.6
  40.3 0.7 fusion.31
  41.0 21.1 %collective-permute-done = bf16[1024,512]{1,0:T(8,128)(2,1)S(1)} collective-permute-done((bf16[1024,512]{1,0:T(8,128)(2,1)S(1)}, bf16[1024,512]{1,0:T(8,128)(2,1)S(1)}, u32[]{:S(2)}, u32[]{:S(2)}) %collective-permute-start) | collective-permute-done | bytes 1048608 | tf_op jit(solution)/shard_map/ppermute | solution.py:13
  62.1 1.4 convolution_multiply_fusion
  63.8 1.6 select_reduce_fusion.1
  66.0 3.3 %multiply_reduce_fusion = (f32[]{:T(128)}, f32[512,512]{1,0:T(8,128)S(1)}) fusion(f32[]{:T(128)S(6)} %mul_shard_map.3, f32[512,512]{1,0:T(8,128)S(1)} %convolution_multiply_fusion, f32[512,512]{0,1:T(8,128)S(1)} %copy.26, pred[]{:T(512)} %bitcast.1), kind=kOutput, calls=%fused_computation.23 | convolution fusion | flops 1612185600 | bytes 3145737 | tf_op jit(solution)/shard_map/dot_general | solution.py:17
  70.0 2.0 %fusion.7 = f32[512,512]{1,0:T(8,128)S(1)} fusion(f32[512,512]{1,0:T(8,128)S(1)} %get-tuple-element.15, f32[]{:T(128)S(6)} %sqrt.6), kind=kOutput, calls=%fused_computation.19 | convolution fusion | flops 1611923456 | bytes 2097156 | tf_op jit(solution)/shard_map/dot_general | solution.py:17
  72.0 1.8 fusion.51
  73.8 1.9 fusion.50
  75.7 1.9 %fusion.14 = f32[512,512]{1,0:T(8,128)S(1)} fusion(f32[512,512]{1,0:T(8,128)S(1)} %fusion.50), kind=kOutput, calls=%fused_computation.30 | convolution fusion | flops 1611661312 | bytes 2097152 | tf_op jit(solution)/shard_map/dot_general | solution.py:17
  77.6 1.8 fusion.52
  79.5 2.0 %fusion = f32[512,512]{1,0:T(8,128)S(1)} fusion(f32[512,512]{1,0:T(8,128)S(1)} %fusion.52, f32[512,512]{1,0:T(8,128)S(1)} %fusion.50), kind=kOutput, calls=%fused_computation.7 | convolution fusion | flops 1611661312 | bytes 3145728 | tf_op jit(solution)/shard_map/dot_general | solution.py:17
  81.6 3.5 %fusion.9 = f32[512,512]{1,0:T(8,128)S(1)} fusion(f32[512,512]{1,0:T(8,128)} %copy-done.1, f32[]{:T(128)S(6)} %mul.63, f32[512,512]{1,0:T(8,128)} %copy-done.2, f32[]{:T(128)S(6)} %sqrt.6), kind=kOutput, calls=%fused_computation.21 | convolution fusion | flops 1612972032 | bytes 3145736 | tf_op jit(solution)/shard_map/dot_general | solution.py:17
  85.2 1.8 fusion.53
  87.0 1.6 collective-permute-start.1
  91.8 18.1 %collective-permute-done.1 = f32[512,512]{1,0:T(8,128)S(1)} collective-permute-done((f32[512,512]{1,0:T(8,128)S(1)}, f32[512,512]{1,0:T(8,128)S(1)}, u32[]{:S(2)}, u32[]{:S(2)}) %collective-permute-start.1) | collective-permute-done | bytes 1048608 | tf_op jit(solution)/shard_map/ppermute | solution.py:13
  110.0 2.5 %fusion.3 = f32[512,512]{1,0:T(8,128)S(1)} fusion(f32[512,512]{1,0:T(8,128)S(1)} %convolution_multiply_fusion, f32[512,512]{1,0:T(8,128)S(1)} %collective-permute-done.1, f32[512,512]{1,0:T(8,128)S(1)} %fusion.53, pred[]{:T(512)} %bitcast.1), kind=kOutput, calls=%fused_computation.15 | convolution fusion | flops 1610874880 | bytes 4194305 | tf_op jit(solution)/shard_map/dot_general | solution.py:17
  112.5 2.5 %select_reduce_fusion = (f32[512]{0:T(512)S(1)}, f32[512,512]{1,0:T(8,128)S(1)}) fusion(pred[512]{0:T(512)(128)(4,1)S(1)} %fusion.31, f32[512,512]{1,0:T(8,128)S(1)} %fusion.3, f32[512,512]{1,0:T(8,128)S(1)} %fusion.53, f32[512,512]{1,0:T(8,128)S(1)} %collective-permute-done.1, pred[]{:T(512)} %bitcast.1), kind=kOutput, calls=%fused_computation.14 | convolution fusion | flops 1611660800 | bytes 4196865 | tf_op jit(solution)/shard_map/dot_general | solution.py:17
  115.0 39.3 %all-reduce = (f32[512]{0:T(512)S(1)}, f32[512]{0:T(512)S(1)}) all-reduce(f32[512]{0:T(512)S(1)} %get-tuple-element.4, f32[512]{0:T(512)S(1)} %get-tuple-element.16), channel_id=1, replica_groups=mesh['dp'=8,'mp'=4] {'dp','mp'}, use_global_device_ids=true, to_apply=%region_3.5 | all-reduce | flops 1024 | bytes 8192 | tf_op jit(solution)/shard_map/psum | solution.py:78
  154.4 0.6 reduce_sum.69
  155.6 0.6 reduce_sum.65
  156.9 0.8 select_convert_fusion
  157.8 29.7 %all_to_all.21 = bf16[8,128,512]{2,1,0:T(8,128)(2,1)S(1)} all-to-all(bf16[8,128,512]{2,1,0:T(8,128)(2,1)S(1)} %constant_dynamic-update-slice_fusion), channel_id=1, replica_groups=mesh['dp'=8,'mp'=4] {'dp'}, dimensions={0} | all-to-all | bytes 2097152 | tf_op jit(solution)/shard_map/all_to_all | solution.py:94
  187.6 0.7 convolution_convert_fusion
  188.3 0.7 copy.28
  (23 shorter events, 2.0 us)
Async XLA Ops:
  0.6 0.7 copy-start.4
  2.7 1.0 copy-start.3
  38.3 23.7 %collective-permute-start = (bf16[1024,512]{1,0:T(8,128)(2,1)S(1)}, bf16[1024,512]{1,0:T(8,128)(2,1)S(1)}, u32[]{:S(2)}, u32[]{:S(2)}) collective-permute-start(bf16[1024,512]{1,0:T(8,128)(2,1)S(1)} %bitcast.39), channel_id=1, source_target_pairs={{0,4},{4,0},{8,12},{12,8},{16,20},{20,16},{24,28},{28,24},{1,5},{5... | collective-permute-start | bytes 3145736 | tf_op jit(solution)/shard_map/ppermute | solution.py:13
  69.3 4.5 %copy-start.2 = (f32[512,512]{1,0:T(8,128)}, f32[512,512]{1,0:T(8,128)S(1)}, u32[]{:S(2)}) copy-start(f32[512,512]{1,0:T(8,128)S(1)} %get-tuple-element.15) | copy-start | bytes 3145732
  75.7 3.8 %copy-start.1 = (f32[512,512]{1,0:T(8,128)}, f32[512,512]{1,0:T(8,128)S(1)}, u32[]{:S(2)}) copy-start(f32[512,512]{1,0:T(8,128)S(1)} %fusion.50) | copy-start | bytes 3145732
  87.0 25.5 %copy-start = (f32[512,512]{1,0:T(8,128)}, f32[512,512]{1,0:T(8,128)S(1)}, u32[]{:S(2)}) copy-start(f32[512,512]{1,0:T(8,128)S(1)} %fusion.53) | copy-start | bytes 3145732
  87.0 22.9 %collective-permute-start.1 = (f32[512,512]{1,0:T(8,128)S(1)}, f32[512,512]{1,0:T(8,128)S(1)}, u32[]{:S(2)}, u32[]{:S(2)}) collective-permute-start(f32[512,512]{1,0:T(8,128)S(1)} %fusion.53), channel_id=1, source_target_pairs={{0,4},{4,0},{8,12},{12,8},{16,20},{20,16},{24,28},{28,24},{1,5},{5... | collective-permute-start | bytes 3145736 | tf_op jit(solution)/shard_map/ppermute | solution.py:13
where the time goes:
time: 191 us; the launch traced here: 190 us
  blocking collectives  102 us (53%)
  waiting for transfers between devices  39.2 us (21%)
  matrix products  27.3 us (14%)
  between operations  7.38 us (4%)
  local copies, waits for them, and re-layouts  5.98 us (3%)
  other arithmetic  5.36 us (3%)
  starting transfers between devices  3.01 us (2%)
    psum x1, blocking collectives, on_device(): grad_total = jnp.sum(lax.psum(grad_share, ('dp', 'mp')))  39.3 us
    ppermute x2, waiting for transfers between devices, partner_2(): lax.ppermute(value, axis, [(i, i ^ 1 << bit) for i in range(lax.axis_size...  39.2 us
    all_to_all x1, blocking collectives, on_device(): lax.all_to_all(mixed, 'dp', split_axis=1, concat_axis=0, tiled=True)  32.8 us
    all_to_all x1, blocking collectives, on_device(): lax.all_to_all(outgoing, 'dp', split_axis=0, concat_axis=0, tiled=True)  29.7 us
    dot_general x11, matrix products, product(): jnp.dot(left, right, precision=lax.Precision.HIGHEST, preferred_element_t...  25.2 us
  transfers between devices with their start and end apart: 2, of which 2 were waited for; matrix products, arithmetic and copies ran while one was open for 1% of the time, Pallas kernels for 0%

commit v1 on v0

--- a/solution.py
+++ b/solution.py
@@ -75,7 +75,7 @@
         inputs_block, outputs_block, (((0,), (0,)), ((), ())), preferred_element_type=jnp.float32
     ) / math.sqrt(all_tokens)
     grad_share = half_squares(gradient, my_left)
-    grad_total = jnp.sum(lax.psum(grad_share, ("dp", "mp")))
+    grad_total = jnp.sum(lax.psum(lax.psum(grad_share, axis_name="mp"), axis_name="dp"))
     oriented = jnp.where(my_left, gradient, gradient.T)
     root = inverse_root(statistic_of(oriented))
     other_root = partner_2(root, "dp", 0)

time: 191 us -> 203 us (1.063)
  blocking collectives: 102 us -> 132 us
  waiting for transfers between devices: 39.2 us -> 21.1 us
    psum x1 -> x3, blocking collectives: 39.3 us -> 68.8 us  [the longest x1 36.9 us: on_device(): precond_total = jnp.sum(lax.psum(precond_share, ('dp', 'mp')))]
    ppermute x2, waiting for transfers between devices: 39.2 us -> 21.1 us  [partner_2(): lax.ppermute(value, axis, [(i, i ^ 1 << bit) for i in range(lax.axis_size...]
  transfers between devices with their start and end apart: 2 -> 2, of which waited for: 2 -> 1; matrix products, arithmetic and copies ran while one was open for 1% -> 1% of each run, Pallas kernels for 0% -> 0%
where the time goes in v1:
time: 203 us
  blocking collectives  132 us (65%)
  matrix products  27.3 us (13%)
  waiting for transfers between devices  21.1 us (10%)
  between operations  7.42 us (4%)
  local copies, waits for them, and re-layouts  5.98 us (3%)
  other arithmetic  5.45 us (3%)
  starting transfers between devices  3.01 us (1%)
    psum x1, blocking collectives, on_device(): precond_total = jnp.sum(lax.psum(precond_share, ('dp', 'mp')))  36.9 us
    all_to_all x1, blocking collectives, on_device(): lax.all_to_all(mixed, 'dp', split_axis=1, concat_axis=0, tiled=True)  32.8 us
    all_to_all x1, blocking collectives, on_device(): lax.all_to_all(outgoing, 'dp', split_axis=0, concat_axis=0, tiled=True)  30.8 us
    psum x1, blocking collectives, on_device(): lax.psum(lax.psum(grad_share, axis_name='mp'), axis_name='dp')  25.9 us
    dot_general x11, matrix products, product(): jnp.dot(left, right, precision=lax.Precision.HIGHEST, preferred_element_t...  25.2 us
    ppermute x2, waiting for transfers between devices, partner_2(): lax.ppermute(value, axis, [(i, i ^ 1 << bit) for i in range(lax.axis_size...  21.1 us
    psum x1, blocking collectives, on_device(): lax.psum(grad_share, axis_name='mp')  5.96 us
  transfers between devices with their start and end apart: 2, of which 1 were waited for; matrix products, arithmetic and copies ran while one was open for 1% of the time, Pallas kernels for 0%

profile of v1, /device:TPU:0, one launch (start us, length us, event | category | flops | bytes accessed | tf_op | source)
XLA Modules:
  0.0 202.7 jit_solution(10443683498046460602)
XLA Ops:
  0.6 0.7 fusion.38
  1.6 1.1 copy.24
  2.9 0.8 copy-done.3
  4.0 0.6 gather_fusion.1
  4.6 0.6 gather_fusion
  5.5 32.8 %all_to_all.20 = bf16[128,8,512]{2,0,1:T(8,128)(2,1)S(1)} all-to-all(bf16[128,8,512]{2,0,1:T(8,128)(2,1)S(1)} %bitcast_select_fusion.1), channel_id=1, replica_groups=mesh['dp'=8,'mp'=4] {'dp'}, dimensions={1} | all-to-all | bytes 2097152 | tf_op jit(solution)/shard_map/all_to_all | solution.py:69
  38.3 1.4 collective-permute-start
  40.3 0.7 fusion.31
  41.0 21.1 %collective-permute-done = bf16[1024,512]{1,0:T(8,128)(2,1)S(1)} collective-permute-done((bf16[1024,512]{1,0:T(8,128)(2,1)S(1)}, bf16[1024,512]{1,0:T(8,128)(2,1)S(1)}, u32[]{:S(2)}, u32[]{:S(2)}) %collective-permute-start) | collective-permute-done | bytes 1048608 | tf_op jit(solution)/shard_map/ppermute | solution.py:13
  62.1 1.4 convolution_multiply_fusion
  63.8 1.6 select_reduce_fusion.1
  66.0 3.3 %multiply_reduce_fusion = (f32[]{:T(128)}, f32[512,512]{1,0:T(8,128)S(1)}) fusion(f32[]{:T(128)S(6)} %mul_shard_map.3, f32[512,512]{1,0:T(8,128)S(1)} %convolution_multiply_fusion, f32[512,512]{0,1:T(8,128)S(1)} %copy.26, pred[]{:T(512)} %bitcast.1), kind=kOutput, calls=%fused_computation.23 | convolution fusion | flops 1612185600 | bytes 3145737 | tf_op jit(solution)/shard_map/dot_general | solution.py:17
  70.0 2.0 fusion.7
  72.0 1.8 fusion.51
  73.8 1.9 fusion.50
  75.7 1.9 fusion.14
  77.6 1.8 fusion.52
  79.5 2.0 %fusion = f32[512,512]{1,0:T(8,128)S(1)} fusion(f32[512,512]{1,0:T(8,128)S(1)} %fusion.52, f32[512,512]{1,0:T(8,128)S(1)} %fusion.50), kind=kOutput, calls=%fused_computation.7 | convolution fusion | flops 1611661312 | bytes 3145728 | tf_op jit(solution)/shard_map/dot_general | solution.py:17
  81.6 3.5 %fusion.9 = f32[512,512]{1,0:T(8,128)S(1)} fusion(f32[512,512]{1,0:T(8,128)} %copy-done.1, f32[]{:T(128)S(6)} %mul.63, f32[512,512]{1,0:T(8,128)} %copy-done.2, f32[]{:T(128)S(6)} %sqrt.6), kind=kOutput, calls=%fused_computation.21 | convolution fusion | flops 1612972032 | bytes 3145736 | tf_op jit(solution)/shard_map/dot_general | solution.py:17
  85.2 1.8 fusion.53
  87.0 1.6 collective-permute-start.1
  91.8 6.0 %psum.21 = f32[512]{0:T(512)S(1)} all-reduce(f32[512]{0:T(512)S(1)} %get-tuple-element.4), channel_id=1, replica_groups=mesh['dp'=8,'mp'=4] {'mp'}, use_global_device_ids=true, to_apply=%region_3.5 | all-reduce | flops 512 | bytes 4096 | tf_op jit(solution)/shard_map/psum | solution.py:78
  97.8 25.9 %psum.22 = f32[512]{0:T(512)S(1)} all-reduce(f32[512]{0:T(512)S(1)} %psum.21), channel_id=1, replica_groups=mesh['dp'=8,'mp'=4] {'dp'}, use_global_device_ids=true, to_apply=%region_4.6 | all-reduce | flops 512 | bytes 4096 | tf_op jit(solution)/shard_map/psum | solution.py:78
  123.7 0.6 reduce_sum.65
  124.3 2.5 %fusion.3 = f32[512,512]{1,0:T(8,128)S(1)} fusion(f32[512,512]{1,0:T(8,128)S(1)} %convolution_multiply_fusion, f32[512,512]{1,0:T(8,128)S(1)} %collective-permute-done.1, f32[512,512]{1,0:T(8,128)S(1)} %fusion.53, pred[]{:T(512)} %bitcast.1), kind=kOutput, calls=%fused_computation.15 | convolution fusion | flops 1610874880 | bytes 4194305 | tf_op jit(solution)/shard_map/dot_general | solution.py:17
  126.9 2.5 %select_reduce_fusion = (f32[512]{0:T(512)S(1)}, f32[512,512]{1,0:T(8,128)S(1)}) fusion(pred[512]{0:T(512)(128)(4,1)S(1)} %fusion.31, f32[512,512]{1,0:T(8,128)S(1)} %fusion.3, f32[512,512]{1,0:T(8,128)S(1)} %fusion.53, f32[512,512]{1,0:T(8,128)S(1)} %collective-permute-done.1, pred[]{:T(512)} %bitcast.1), kind=kOutput, calls=%fused_computation.14 | convolution fusion | flops 1611660800 | bytes 4196865 | tf_op jit(solution)/shard_map/dot_general | solution.py:17
  129.4 36.9 %psum.23 = f32[512]{0:T(512)S(1)} all-reduce(f32[512]{0:T(512)S(1)} %get-tuple-element.14), channel_id=1, replica_groups=mesh['dp'=8,'mp'=4] {'dp','mp'}, use_global_device_ids=true, to_apply=%region_9.11 | all-reduce | flops 512 | bytes 4096 | tf_op jit(solution)/shard_map/psum | solution.py:86
  166.3 0.7 reduce_sum.69
  168.3 0.8 select_convert_fusion
  169.3 30.8 %all_to_all.21 = bf16[8,128,512]{2,1,0:T(8,128)(2,1)S(1)} all-to-all(bf16[8,128,512]{2,1,0:T(8,128)(2,1)S(1)} %constant_dynamic-update-slice_fusion), channel_id=1, replica_groups=mesh['dp'=8,'mp'=4] {'dp'}, dimensions={0} | all-to-all | bytes 2097152 | tf_op jit(solution)/shard_map/all_to_all | solution.py:94
  200.0 0.7 convolution_convert_fusion
  200.8 0.7 copy.28
  (25 shorter events, 2.6 us)
Async XLA Ops:
  0.6 0.7 copy-start.4
  2.7 1.0 copy-start.3
  38.3 23.7 %collective-permute-start = (bf16[1024,512]{1,0:T(8,128)(2,1)S(1)}, bf16[1024,512]{1,0:T(8,128)(2,1)S(1)}, u32[]{:S(2)}, u32[]{:S(2)}) collective-permute-start(bf16[1024,512]{1,0:T(8,128)(2,1)S(1)} %bitcast.39), channel_id=1, source_target_pairs={{0,4},{4,0},{8,12},{12,8},{16,20},{20,16},{24,28},{28,24},{1,5},{5... | collective-permute-start | bytes 3145736 | tf_op jit(solution)/shard_map/ppermute | solution.py:13
  69.3 4.5 %copy-start.2 = (f32[512,512]{1,0:T(8,128)}, f32[512,512]{1,0:T(8,128)S(1)}, u32[]{:S(2)}) copy-start(f32[512,512]{1,0:T(8,128)S(1)} %get-tuple-element.13) | copy-start | bytes 3145732
  75.7 3.8 %copy-start.1 = (f32[512,512]{1,0:T(8,128)}, f32[512,512]{1,0:T(8,128)S(1)}, u32[]{:S(2)}) copy-start(f32[512,512]{1,0:T(8,128)S(1)} %fusion.50) | copy-start | bytes 3145732
  87.0 39.8 %copy-start = (f32[512,512]{1,0:T(8,128)}, f32[512,512]{1,0:T(8,128)S(1)}, u32[]{:S(2)}) copy-start(f32[512,512]{1,0:T(8,128)S(1)} %fusion.53) | copy-start | bytes 3145732
  87.0 37.3 %collective-permute-start.1 = (f32[512,512]{1,0:T(8,128)S(1)}, f32[512,512]{1,0:T(8,128)S(1)}, u32[]{:S(2)}, u32[]{:S(2)}) collective-permute-start(f32[512,512]{1,0:T(8,128)S(1)} %fusion.53), channel_id=1, source_target_pairs={{0,4},{4,0},{8,12},{12,8},{16,20},{20,16},{24,28},{28,24},{1,5},{5... | collective-permute-start | bytes 3145736 | tf_op jit(solution)/shard_map/ppermute | solution.py:13
